TPU v7x, 32 devices: a whole 2x2x4 slice. The times are simulated.
32 devices in a mesh: gx: 8 (over y, x, core), gy: 4 (over z).
Axes of the slice: x: 2, y: 2, z: 4, core: 2. Of those that a mesh axis runs over, the one named last changes fastest.
Arguments:
- modes: bfloat16 [256, 128, 4, 3, 256], P('gx', 'gy'), may hold values from -6 to 6
- adv_index: int32 [8], replicated, may hold values from 0 to 255
Outputs:
- convection: float32 [256, 8, 256], P('gx', None, 'gy')
All inputs are finite; a program needn't handle non-finite values.
Results may differ from a plain program's by a relative error of at most 0.0041.
Values may be sent and summed in bfloat16 or wider, within the bound.
A program may use at most 192 MiB of HBM per device.

v0:
```python
import math

import jax
import jax.numpy as jnp
from jax import lax
from jax.sharding import PartitionSpec as P

BATCHES = 2


def with_halo(cells, sides, width):
    for axis, dim in sides:
        count = lax.axis_size(axis)
        head = lax.slice_in_dim(cells, 0, width, axis=dim)
        tail = lax.slice_in_dim(cells, cells.shape[dim] - width, cells.shape[dim], axis=dim)
        cells = jnp.concatenate(
            [
                lax.ppermute(tail, axis, [(i, (i + 1) % count) for i in range(count)]),
                cells,
                lax.ppermute(head, axis, [((i + 1) % count, i) for i in range(count)]),
            ],
            axis=dim,
        )
    return cells


def difference(padded, axis):
    length = padded.shape[axis] - 4

    def shifted(offset):
        return lax.slice_in_dim(padded, offset, offset + length, axis=axis).astype(jnp.float32)

    return (shifted(0) - shifted(4) + 8.0 * (shifted(3) - shifted(1))) / 12.0


def per_device(modes, adv_index):
    cells_x, cells_y, cells_z, components, width = modes.shape
    rimmed = with_halo(modes, (("gx", 0), ("gy", 1)), 2)
    rimmed = jnp.pad(rimmed, ((0, 0), (0, 0), (2, 2), (0, 0), (0, 0)))
    grad_x = difference(rimmed[:, 2:-2, 2:-2], 0).astype(jnp.bfloat16)
    grad_y = difference(rimmed[2:-2, :, 2:-2], 1).astype(jnp.bfloat16)
    grad_z = difference(rimmed[2:-2, 2:-2, :], 2).astype(jnp.bfloat16)
    advect = jnp.take(modes, adv_index, axis=4).astype(jnp.float32)
    flat = modes.reshape(-1, width)
    advecting = adv_index.shape[0]
    per_portion = advecting // BATCHES
    groups_x = lax.axis_size("gx")
    groups_y = lax.axis_size("gy")
    factor = 1.0 / math.sqrt(3.0 * cells_x * cells_y * cells_z * groups_x * groups_y)

    def convect(column):
        speed_x = advect[:, :, :, 0, column][..., None, None]
        speed_y = advect[:, :, :, 1, column][..., None, None]
        speed_z = advect[:, :, :, 2, column][..., None, None]
        field = speed_x * grad_x + speed_y * grad_y + speed_z * grad_z
        field = field.astype(jnp.bfloat16).reshape(-1, width)
        return lax.dot_general(
            flat, field, (((0,), (0,)), ((), ())), preferred_element_type=jnp.float32
        )

    results = []
    for portion in range(BATCHES):
        columns = [
            convect(column) for column in range(portion * per_portion, (portion + 1) * per_portion)
        ]
        partial_value = jnp.stack(columns, axis=1)
        owned = lax.psum_scatter(partial_value, "gy", scatter_dimension=2, tiled=True)
        owned = lax.psum_scatter(owned, "gx", scatter_dimension=0, tiled=True)
        results.append(owned)
    return jnp.concatenate(results, axis=1) * factor


def solution(mesh):
    return jax.shard_map(
        per_device,
        mesh=mesh,
        in_specs=(P("gx", "gy", None, None, None), P()),
        out_specs=P("gx", None, "gy"),
        check_vma=False,
    )
```

profile of v0, /device:TPU:0, one launch (start us, length us, event | category | flops | bytes accessed | tf_op | source)
XLA Modules:
  0.0 368.7 jit_solution(12879941140484022588)
XLA Ops:
  6.5 2.1 fusion.81
  9.2 2.9 collective-permute-start.1
  12.1 41.0 %copy.62 = bf16[32,32,4,3,256]{1,0,3,2,4:T(8,128)(2,1)} copy(bf16[32,32,4,3,256]{4,2,3,1,0:T(4,128)(2,1)} %param.2) | data formatting | bytes 12582912 | tf_op args[0]
  53.1 8.9 %gather_fusion = bf16[8,32,32,4,3]{2,1,4,3,0:T(8,128)(2,1)S(1)} fusion(bf16[32,32,4,3,256]{1,0,3,2,4:T(8,128)(2,1)} %copy.62, s32[1024]{0:T(1024)S(1)} %pad_clamp_fusion), kind=kCustom, calls=%fused_computation | custom fusion | bytes 393248 | tf_op jit(solution)/shard_map/jit(_take)/gather | solution.py:43
  62.4 13.2 %constant_dynamic-update-slice_fusion.3 = (bf16[34,32,4,3,256]{4,2,3,1,0:T(4,128)(2,1)}, bf16[34,32,4,3,256]{4,2,3,1,0:T(4,128)(2,1)S(1)}, bf16[36,32,4,3,256]{4,2,3,1,0:T(4,128)(2,1)S(1)}) fusion(bf16[32,32,4,3,256]{4,2,3,1,0:T(4,128)(2,1)} %param.2, bf16[34,32,4,3,256]{4,2,3,1,0:T(4,128)(2,1)S(1)} %get-tuple-element.51, ...), kind=kLoop, calls=%fused_computation.131 | loop fusion | bytes 25165824
  75.6 1.3 constant_dynamic-update-slice_fusion.2
  76.8 3.2 copy-done.2
  80.1 1.2 fusion.80
  81.3 2.3 collective-permute-start.2
  83.7 2.0 collective-permute-start.3
  86.3 1.1 copy.65
  88.2 2.0 copy.68
  90.2 1.9 copy.73
  92.1 1.9 copy.74
  94.0 1.9 copy.75
  95.9 1.9 copy.78
  97.9 1.9 copy.79
  99.8 1.9 copy.80
  101.7 1.9 copy.84
  103.6 1.9 copy.85
  105.5 1.9 copy.86
  107.4 1.9 copy.89
  109.3 1.9 copy.90
  111.2 1.1 copy.91
  113.4 1.1 copy.70
  114.5 1.1 copy.100
  115.5 1.1 copy.101
  116.6 1.1 copy.94
  117.7 1.1 copy.95
  118.8 1.1 copy.96
  119.8 1.1 copy.99
  120.9 13.9 %fusion.5 = bf16[36,36,8,3,256]{4,2,3,1,0:T(8,128)(2,1)} fusion(bf16[36,2,4,3,256]{4,2,3,1,0:T(4,128)(2,1)} %collective-permute-done.3, bf16[36,32,4,3,256]{4,2,3,1,0:T(4,128)(2,1)} %copy-done.2, bf16[36,2,4,3,256]{4,2,3,1,0:T(4,128)(2,1)S(1)} %collective-permute-done.2), kind=kLoop, calls=%fused_computation.32 | loop fusion | flops 95551488 | bytes 23887872 | tf_op jit(solution)/shard_map/concatenate | solution.py:16
  134.8 56.1 %fusion.8 = (bf16[32,32,4,3,256]{4,2,3,1,0:T(4,128)(2,1)}, bf16[32,32,4,3,256]{4,2,3,1,0:T(4,128)(2,1)S(1)}, bf16[32,32,4,3,256]{4,2,3,1,0:T(4,128)(2,1)S(1)}, bf16[32,32,4,3,256]{4,2,3,1,0:T(4,128)(2,1)}) fusion(f32[32,32,4]{2,1,0:T(8,128)S(1)} %copy-done.5, f32[32,32,4]{2,1,0:T(8,128)S(1)} %copy.64, f32[32,32,4]{2,1,0:T(8,128)S(1)} %copy.63, ...), kind=kLoop, calls=%fused_computation.35 | loop fusion | flops 135266304 | bytes 83509248 | tf_op jit(solution)/shard_map/convert_element_type | solution.py:56
  190.9 35.2 %fusion.11 = (bf16[32,32,4,3,256]{4,2,3,1,0:T(4,128)(2,1)S(1)}, bf16[32,32,4,3,256]{4,2,3,1,0:T(4,128)(2,1)}, bf16[32,32,4,3,256]{4,2,3,1,0:T(4,128)(2,1)}, bf16...) fusion(bf16[32,32,4,3,256]{4,2,3,1,0:T(4,128)(2,1)} %get-tuple-element.10, ...), kind=kLoop, calls=%fused_computation.38 | loop fusion | flops 103809024 | bytes 50577408 | tf_op jit(solution)/shard_map/convert_element_type | solution.py:56
  226.2 4.8 %fusion.51 = f32[256,1,256]{0,2,1:T(8,128)S(1)} fusion(bf16[32,32,4,3,256]{4,2,3,1,0:T(4,128)(2,1)S(1)} %get-tuple-element.11, bf16[32,32,4,3,256]{4,2,3,1,0:T(4,128)(2,1)} %param.2), kind=kOutput, calls=%fused_computation.86 | convolution fusion | flops 1610612736 | bytes 12845056 | tf_op jit(solution)/shard_map/dot_general | solution.py:57
  231.0 5.4 %fusion.54 = f32[256,1,256]{0,2,1:T(8,128)S(1)} fusion(bf16[32,32,4,3,256]{4,2,3,1,0:T(4,128)(2,1)S(1)} %copy-done.4, bf16[32,32,4,3,256]{4,2,3,1,0:T(4,128)(2,1)} %param.2), kind=kOutput, calls=%fused_computation.87 | convolution fusion | flops 1610612736 | bytes 12845056 | tf_op jit(solution)/shard_map/dot_general | solution.py:57
  236.5 1.8 fusion.57
  238.3 1.8 fusion.48
  241.6 6.7 %fusion.60 = f32[256,1,256]{0,2,1:T(8,128)S(1)} fusion(bf16[32,32,4,3,256]{4,2,3,1,0:T(4,128)(2,1)} %get-tuple-element.14, bf16[32,32,4,3,256]{4,2,3,1,0:T(4,128)(2,1)} %param.2), kind=kOutput, calls=%fused_computation.89 | convolution fusion | flops 1610612736 | bytes 12845056 | tf_op jit(solution)/shard_map/dot_general | solution.py:57
  248.5 16.0 %fusion.26 = (bf16[32,32,4,3,256]{4,2,3,1,0:T(4,128)(2,1)S(1)}, bf16[32,32,4,3,256]{4,2,3,1,0:T(4,128)(2,1)S(1)}) fusion(bf16[32,32,4,3,256]{4,2,3,1,0:T(4,128)(2,1)} %get-tuple-element.10, bf16[32,32,4,3,256]{4,2,3,1,0:T(4,128)(2,1)} %copy-done.1, bf16[32,32,4,3,256]{4,2,3,1,0:T(4,128)(2,1)S(1)} %bitcast.116, f32[32,32,4]{2,1,0:T(8,128)S(1)} %copy-done.10, ...), kind=kLoop, calls=%fused_computation.53 | loop fusion | flops 47185920 | bytes 31555584 | tf_op jit(solution)/shard_map/convert_element_type | solution.py:56
  264.5 6.6 %fusion.63 = f32[256,1,256]{0,2,1:T(8,128)S(1)} fusion(bf16[32,32,4,3,256]{4,2,3,1,0:T(4,128)(2,1)} %get-tuple-element.15, bf16[32,32,4,3,256]{4,2,3,1,0:T(4,128)(2,1)} %param.2), kind=kOutput, calls=%fused_computation.90 | convolution fusion | flops 1610612736 | bytes 12845056 | tf_op jit(solution)/shard_map/dot_general | solution.py:57
  271.2 1.8 fusion.66
  273.0 1.8 fusion.69
  274.9 1.1 pad_maximum_fusion.3
  276.0 2.0 copy.83
  278.0 24.1 %reduce-scatter.5.cloned.1.call-done = f32[256,4,64]{0,2,1:T(8,128)} async-done(((f32[256,4,256]{0,2,1:T(8,128)}), f32[256,4,64]{0,2,1:T(8,128)}) %reduce-scatter.5.cloned.1.call-update) | async-done | bytes 262160 | tf_op jit(solution)/shard_map/reduce_scatter | solution.py:67
  302.1 2.0 copy.104
  305.3 55.3 %all-reduce.6.cloned.1.call-done = (f32[256,4,64]{2,1,0:T(4,128)}, f32[256,4,64]{2,1,0:T(4,128)}) async-done(((f32[256,4,64]{2,1,0:T(4,128)}, f32[256,4,64]{2,1,0:T(4,128)}), (f32[256,4,64]{2,1,0:T(4,128)}, f32[256,4,64]{2,1,0:T(4,128)})) %all-reduce.6.cloned.1.call-update) | async-done | bytes 524304
  (84 shorter events, 7.3 us)
Async XLA Ops:
  6.5 269.5 %reduce-scatter.3.cloned.1.call-start = ((), (), s32[]{:S(2)}) async-start(), calls=%async_computation.2 | async-start | bytes 1310720 | tf_op jit(solution)/shard_map/reduce_scatter | solution.py:67
  8.7 53.5 %collective-permute-start = (bf16[2,32,4,3,256]{4,2,3,1,0:T(4,128)(2,1)}, bf16[2,32,4,3,256]{4,2,3,1,0:T(4,128)(2,1)S(1)}, u32[]{:S(2)}, u32[]{:S(2)}) collective-permute-start(bf16[2,32,4,3,256]{4,2,3,1,0:T(4,128)(2,1)} %get-tuple-element.24), channel_id=1, source_target_pairs={{0,4},{4,8},{8,12},{12,16},{16,20},{20,24},{24,28},{28,0},{1,5},{5... | collective-permute-start | bytes 1179656 | tf_op jit(solution)/shard_map/ppermute | solution.py:18
  9.2 43.9 %copy-start.15 = (s32[8]{0:T(128)S(1)}, s32[8]{0:T(128)}, u32[]{:S(2)}) copy-start(s32[8]{0:T(128)} %param.3) | copy-start | bytes 100
  9.2 66.4 %collective-permute-start.1 = (bf16[2,32,4,3,256]{4,2,3,1,0:T(4,128)(2,1)S(1)}, bf16[2,32,4,3,256]{4,2,3,1,0:T(4,128)(2,1)S(1)}, u32[]{:S(2)}, u32[]{:S(2)}) collective-permute-start(bf16[2,32,4,3,256]{4,2,3,1,0:T(4,128)(2,1)S(1)} %get-tuple-element.23), channel_id=1, source_target_pairs={{4,0},{8,4},{12,8},{16,12},{20,16},{24,20},{28,24},{0,28},{5,1},{9... | collective-permute-start | bytes 1179656 | tf_op jit(solution)/shard_map/ppermute | solution.py:20
  75.5 5.8 %copy-start.3 = (bf16[34,32,4,3,256]{4,2,3,1,0:T(4,128)(2,1)}, bf16[34,32,4,3,256]{4,2,3,1,0:T(4,128)(2,1)S(1)}, u32[]{:S(2)}) copy-start(bf16[34,32,4,3,256]{4,2,3,1,0:T(4,128)(2,1)S(1)} %get-tuple-element.21) | copy-start | bytes 20054020
  76.8 3.2 copy-start.2
  81.3 39.6 %collective-permute-start.2 = (bf16[36,2,4,3,256]{4,2,3,1,0:T(4,128)(2,1)}, bf16[36,2,4,3,256]{4,2,3,1,0:T(4,128)(2,1)S(1)}, u32[]{:S(2)}, u32[]{:S(2)}) collective-permute-start(bf16[36,2,4,3,256]{4,2,3,1,0:T(4,128)(2,1)} %get-tuple-element.18), channel_id=1, source_target_pairs={{0,1},{1,2},{2,3},{3,0},{4,5},{5,6},{6,7},{7,4},{8,9},{9,10},{10,1... | collective-permute-start | bytes 1327112 | tf_op jit(solution)/shard_map/ppermute | solution.py:18
  83.7 37.3 %collective-permute-start.3 = (bf16[36,2,4,3,256]{4,2,3,1,0:T(4,128)(2,1)}, bf16[36,2,4,3,256]{4,2,3,1,0:T(4,128)(2,1)}, u32[]{:S(2)}, u32[]{:S(2)}) collective-permute-start(bf16[36,2,4,3,256]{4,2,3,1,0:T(4,128)(2,1)} %get-tuple-element.19), channel_id=1, source_target_pairs={{1,0},{2,1},{3,2},{0,3},{5,4},{6,5},{7,6},{4,7},{9,8},{10,9},{11,1... | collective-permute-start | bytes 1327112 | tf_op jit(solution)/shard_map/ppermute | solution.py:20
  88.2 23.0 %copy-start.14 = (f32[32,32,4]{1,0,2:T(8,128)S(1)}, f32[32,32,4]{1,0,2:T(8,128)}, u32[]{:S(2)}) copy-start(f32[32,32,4]{1,0,2:T(8,128)} %get-tuple-element.32) | copy-start | bytes 49156
  88.2 26.2 %copy-start.13 = (f32[32,32,4]{1,0,2:T(8,128)S(1)}, f32[32,32,4]{1,0,2:T(8,128)}, u32[]{:S(2)}) copy-start(f32[32,32,4]{1,0,2:T(8,128)} %get-tuple-element.27) | copy-start | bytes 49156
  120.9 13.9 %copy-start.5 = (f32[32,32,4]{2,1,0:T(8,128)S(1)}, f32[32,32,4]{2,1,0:T(8,128)}, u32[]{:S(2)}) copy-start(f32[32,32,4]{2,1,0:T(8,128)} %copy.65) | copy-start | bytes 49156
  120.9 13.9 %copy-start.12 = (bf16[36,2,4,3,256]{4,2,3,1,0:T(4,128)(2,1)}, bf16[36,2,4,3,256]{4,2,3,1,0:T(4,128)(2,1)S(1)}, u32[]{:S(2)}) copy-start(bf16[36,2,4,3,256]{4,2,3,1,0:T(4,128)(2,1)S(1)} %collective-permute-done.2) | copy-start | bytes 1327108
  190.9 35.2 %copy-start = (bf16[32,32,4,3,256]{4,2,3,1,0:T(4,128)(2,1)}, bf16[32,32,4,3,256]{4,2,3,1,0:T(4,128)(2,1)S(1)}, u32[]{:S(2)}) copy-start(bf16[32,32,4,3,256]{4,2,3,1,0:T(4,128)(2,1)S(1)} %get-tuple-element.8) | copy-start | bytes 18874372
  190.9 35.2 %copy-start.1 = (bf16[32,32,4,3,256]{4,2,3,1,0:T(4,128)(2,1)}, bf16[32,32,4,3,256]{4,2,3,1,0:T(4,128)(2,1)S(1)}, u32[]{:S(2)}) copy-start(bf16[32,32,4,3,256]{4,2,3,1,0:T(4,128)(2,1)S(1)} %get-tuple-element.9) | copy-start | bytes 18874372
  226.1 4.8 %copy-start.4 = (bf16[32,32,4,3,256]{4,2,3,1,0:T(4,128)(2,1)S(1)}, bf16[32,32,4,3,256]{4,2,3,1,0:T(4,128)(2,1)}, u32[]{:S(2)}) copy-start(bf16[32,32,4,3,256]{4,2,3,1,0:T(4,128)(2,1)} %get-tuple-element.12) | copy-start | bytes 18874372
  226.1 10.3 %slice-start.2 = ((s8[6291456]{0:T(1024)(128)(4,1)}), s8[4194304]{0:T(1024)(128)(4,1)S(1)}, s32[]{:S(2)}) async-start(s8[6291456]{0:T(1024)(128)(4,1)} %bitcast.117), calls=%async_computation.7 | async-start | bytes 8388608
  226.1 10.3 %slice-start.8 = ((s8[6291456]{0:T(1024)(128)(4,1)}), s8[4194304]{0:T(1024)(128)(4,1)S(1)}, s32[]{:S(2)}) async-start(s8[6291456]{0:T(1024)(128)(4,1)} %bitcast.123), calls=%async_computation.13 | async-start | bytes 8388608
  230.9 5.5 %slice-start.3 = ((s8[6291456]{0:T(1024)(128)(4,1)}), s8[2097152]{0:T(1024)(128)(4,1)S(1)}, s32[]{:S(2)}) async-start(s8[6291456]{0:T(1024)(128)(4,1)} %bitcast.117), calls=%async_computation.8 | async-start | bytes 4194304
  231.0 5.5 %slice-start.9 = ((s8[6291456]{0:T(1024)(128)(4,1)}), s8[2097152]{0:T(1024)(128)(4,1)S(1)}, s32[]{:S(2)}) async-start(s8[6291456]{0:T(1024)(128)(4,1)} %bitcast.123), calls=%async_computation.14 | async-start | bytes 4194304
  231.0 7.3 %slice-start.6 = ((s8[6291456]{0:T(1024)(128)(4,1)}), s8[4194304]{0:T(1024)(128)(4,1)S(1)}, s32[]{:S(2)}) async-start(s8[6291456]{0:T(1024)(128)(4,1)} %bitcast.121), calls=%async_computation.11 | async-start | bytes 8388608
  236.5 1.9 slice-start.7
  240.2 8.1 %slice-start = ((s8[6291456]{0:T(1024)(128)(4,1)}), s8[2097152]{0:T(1024)(128)(4,1)S(1)}, s32[]{:S(2)}) async-start(s8[6291456]{0:T(1024)(128)(4,1)} %bitcast.115), calls=%async_computation.5 | async-start | bytes 4194304
  241.3 60.8 %reduce-scatter.5.cloned.1.call-start = ((), (), s32[]{:S(2)}) async-start(), calls=%async_computation.3 | async-start | bytes 1310720 | tf_op jit(solution)/shard_map/reduce_scatter | solution.py:67
  241.5 6.7 %slice-start.1 = ((s8[6291456]{0:T(1024)(128)(4,1)}), s8[4194304]{0:T(1024)(128)(4,1)S(1)}, s32[]{:S(2)}) async-start(s8[6291456]{0:T(1024)(128)(4,1)} %bitcast.115), calls=%async_computation.6 | async-start | bytes 8388608
  241.6 6.7 %copy-start.6 = (f32[32,32,4]{2,1,0:T(8,128)S(1)}, f32[32,32,4]{2,1,0:T(8,128)}, u32[]{:S(2)}) copy-start(f32[32,32,4]{2,1,0:T(8,128)} %copy.100) | copy-start | bytes 49156
  241.6 6.7 %copy-start.7 = (f32[32,32,4]{2,1,0:T(8,128)S(1)}, f32[32,32,4]{2,1,0:T(8,128)}, u32[]{:S(2)}) copy-start(f32[32,32,4]{2,1,0:T(8,128)} %copy.101) | copy-start | bytes 49156
  241.6 6.7 %copy-start.8 = (f32[32,32,4]{2,1,0:T(8,128)S(1)}, f32[32,32,4]{2,1,0:T(8,128)}, u32[]{:S(2)}) copy-start(f32[32,32,4]{2,1,0:T(8,128)} %copy.94) | copy-start | bytes 49156
  241.6 6.7 %copy-start.9 = (f32[32,32,4]{2,1,0:T(8,128)S(1)}, f32[32,32,4]{2,1,0:T(8,128)}, u32[]{:S(2)}) copy-start(f32[32,32,4]{2,1,0:T(8,128)} %copy.95) | copy-start | bytes 49156
  241.6 6.7 %copy-start.10 = (f32[32,32,4]{2,1,0:T(8,128)S(1)}, f32[32,32,4]{2,1,0:T(8,128)}, u32[]{:S(2)}) copy-start(f32[32,32,4]{2,1,0:T(8,128)} %copy.96) | copy-start | bytes 49156
  241.6 6.9 %copy-start.11 = (f32[32,32,4]{2,1,0:T(8,128)S(1)}, f32[32,32,4]{2,1,0:T(8,128)}, u32[]{:S(2)}) copy-start(f32[32,32,4]{2,1,0:T(8,128)} %copy.99) | copy-start | bytes 49156
  248.5 22.6 %slice-start.4 = ((s8[6291456]{0:T(1024)(128)(4,1)}), s8[2097152]{0:T(1024)(128)(4,1)S(1)}, s32[]{:S(2)}) async-start(s8[6291456]{0:T(1024)(128)(4,1)} %bitcast.119), calls=%async_computation.9 | async-start | bytes 4194304
  264.5 6.7 %slice-start.5 = ((s8[6291456]{0:T(1024)(128)(4,1)}), s8[4194304]{0:T(1024)(128)(4,1)S(1)}, s32[]{:S(2)}) async-start(s8[6291456]{0:T(1024)(128)(4,1)} %bitcast.119), calls=%async_computation.10 | async-start | bytes 8388608
  273.0 31.1 %copy-start.16 = (u32[32]{0:T(128)S(1)}, u32[32]{0:T(128)}, u32[]{:S(2)}) copy-start(u32[32]{0:T(128)} %constant.32) | copy-start | bytes 388
  275.9 84.7 %all-reduce.6.cloned.1.call-start = ((), (), s32[]{:S(2)}) async-start(), calls=%async_computation.4 | async-start | bytes 2097152
Sparse Core Ops, SparseCore 0:
  241.4 26.0 reduce-scatter.2
  276.1 25.9 reduce-scatter.4
  305.3 55.2 all-reduce.5
where the time goes:
time: 370 us; the launch traced here: 369 us
  other arithmetic  124 us (34%)
  local copies, waits for them, and re-layouts  112 us (30%)
  waiting for transfers between devices  79.5 us (21%)
  matrix products  30.8 us (8%)
  between operations  14.2 us (4%)
  starting transfers between devices  8.03 us (2%)
    convert_element_type x3, other arithmetic, convect(): field = field.astype(jnp.bfloat16).reshape(-1, width)  107 us
    unnamed x59, local copies, waits for them, and re-layouts  59.4 us
    unnamed x4, waiting for transfers between devices  55.3 us
    mul x26, local copies, waits for them, and re-layouts, convect(): field = speed_x * grad_x + speed_y * grad_y + speed_z * grad_z  35.2 us
    dot_general x8, matrix products, convect(): lax.dot_general(flat, field, (((0,), (0,)), ((), ())), preferred_element_...  30.8 us
    reduce_scatter x2, waiting for transfers between devices, per_device(): lax.psum_scatter(partial_value, 'gy', scatter_dimension=2, tiled=True)  24.1 us
    concatenate x1, other arithmetic, with_halo(): jnp.concatenate([lax.ppermute(tail, axis, [(i, (i + 1) % count) for i in...  13.9 us
    gather x1, local copies, waits for them, and re-layouts, per_device(): advect = jnp.take(modes, adv_index, axis=4).astype(jnp.float32)  8.86 us
  transfers between devices with their start and end apart: 7, of which 2 were waited for; matrix products, arithmetic and copies ran while one was open for 37% of the time, Pallas kernels for 0%

commit v1 on v0

v1 whole, which is shorter than its diff:
```python
import functools
import math

import jax
import jax.numpy as jnp
from jax import lax
from jax.experimental import pallas as pl
from jax.experimental.pallas import tpu as pltpu
from jax.sharding import PartitionSpec as P

PLANES = 2
LANES = 128


def stencil(back2, back1, ahead1, ahead2):
    return (back2 - ahead2 + 8.0 * (ahead1 - back1)) * (1.0 / 12.0)


def prepare(m_ref, pick_ref, turned_ref, speeds_ref, ahead_ref, flat):
    components, cells_z, cells_x, cells_y, width = m_ref.shape
    rows = PLANES * cells_z * cells_y

    def step(block, carry):
        for plane in range(PLANES):
            x = block * PLANES + plane
            for c in range(components):
                centre = [m_ref[c, z, x].astype(jnp.float32) for z in range(cells_z)]
                empty = jnp.zeros_like(centre[0])
                padded = [empty, empty] + centre + [empty, empty]
                for z in range(cells_z):
                    spot = pl.ds((plane * cells_z + z) * cells_y, cells_y)
                    value = stencil(padded[z], padded[z + 1], padded[z + 3], padded[z + 4])
                    ahead_ref[block, c, spot] = value.astype(jnp.bfloat16)
                    flat[c, spot] = m_ref[c, z, x]
        for c in range(components):
            speeds_ref[block, c] = jnp.dot(
                flat[c], pick_ref[...], preferred_element_type=jnp.float32
            ).astype(jnp.bfloat16)
            turned_ref[block, :, c * rows : (c + 1) * rows] = flat[c].T
        return carry

    lax.fori_loop(0, cells_x // PLANES, step, 0)


def kernel(advecting, m_ref, xb_ref, xa_ref, yh_ref, turned_ref, speeds_ref, ahead_ref, out_ref, slab, acc, grads):
    components, cells_z, cells_x, cells_y, width = m_ref.shape
    rows = PLANES * cells_z * cells_y
    tall = cells_y + yh_ref.shape[3]
    acc[...] = jnp.zeros_like(acc)
    slab[:, :, 0:2] = xb_ref[...]
    slab[:, :, cells_x + 2 : cells_x + 4] = xa_ref[...]

    def bring(x, carry):
        slab[:, :, x + 2] = m_ref[:, :, x]
        return carry

    lax.fori_loop(0, cells_x, bring, 0)

    def step(block, carry):
        for plane in range(PLANES):
            x = block * PLANES + plane
            for c in range(components):
                for z in range(cells_z):
                    spot = pl.ds((plane * cells_z + z) * cells_y, cells_y)

                    def along_x(offset):
                        return slab[c, z, x + 2 + offset].astype(jnp.float32)

                    rim = yh_ref[c, z, x].astype(jnp.float32)
                    column = jnp.concatenate([along_x(0), rim], axis=0)

                    def along_y(offset):
                        return pltpu.roll(column, (-offset) % tall, 0)[:cells_y]

                    for d, along in enumerate((along_x, along_y)):
                        value = stencil(along(-2), along(-1), along(1), along(2))
                        grads[d, c, spot] = value.astype(jnp.bfloat16)
        for j in range(advecting):
            speed = [
                jnp.broadcast_to(speeds_ref[block, d, :, j : j + 1].astype(jnp.float32), (rows, width))
                for d in range(3)
            ]
            fields = []
            for c in range(components):
                field = (
                    speed[0] * grads[0, c].astype(jnp.float32)
                    + speed[1] * grads[1, c].astype(jnp.float32)
                    + speed[2] * ahead_ref[block, c].astype(jnp.float32)
                )
                fields.append(field.astype(jnp.bfloat16))
            acc[j] += jnp.dot(
                turned_ref[block], jnp.concatenate(fields, axis=0), preferred_element_type=jnp.float32
            )
        return carry

    lax.fori_loop(0, cells_x // PLANES, step, 0)
    groups, high = out_ref.shape[0], out_ref.shape[1]
    for a in range(groups):
        for j in range(advecting):
            out_ref[a, :, j * width : (j + 1) * width] = acc[j, a * high : (a + 1) * high].astype(jnp.bfloat16)


def convect(inner, before, after, rim, pick, advecting, groups):
    components, cells_z, cells_x, cells_y, width = inner.shape
    rows = PLANES * cells_z * cells_y
    vmem = pl.BlockSpec(memory_space=pltpu.VMEM)
    blocks = cells_x // PLANES
    turned, speeds, ahead = pl.pallas_call(
        prepare,
        out_shape=[
            jax.ShapeDtypeStruct((blocks, width, components * rows), jnp.bfloat16),
            jax.ShapeDtypeStruct((blocks, 3, rows, LANES), jnp.bfloat16),
            jax.ShapeDtypeStruct((blocks, components, rows, width), jnp.bfloat16),
        ],
        in_specs=[vmem] * 2,
        out_specs=[vmem] * 3,
        scratch_shapes=[pltpu.VMEM((components, rows, width), jnp.bfloat16)],
        compiler_params=pltpu.CompilerParams(vmem_limit_bytes=28 * 1024 * 1024),
        cost_estimate=pl.CostEstimate(flops=20_000_000_000, bytes_accessed=30_000_000, transcendentals=0),
        name="prepare",
    )(inner, pick)
    return pl.pallas_call(
        functools.partial(kernel, advecting),
        out_shape=jax.ShapeDtypeStruct((groups, width // groups, advecting * width), jnp.bfloat16),
        in_specs=[vmem] * 7,
        out_specs=vmem,
        scratch_shapes=[
            pltpu.VMEM((components, cells_z, cells_x + 4, cells_y, width), jnp.bfloat16),
            pltpu.VMEM((advecting, width, width), jnp.float32),
            pltpu.VMEM((2, components, rows, width), jnp.bfloat16),
        ],
        compiler_params=pltpu.CompilerParams(vmem_limit_bytes=44 * 1024 * 1024),
        name="convect",
    )(inner, before, after, rim, turned, speeds, ahead)


def neighbours(cells, axis, dim):
    count = lax.axis_size(axis)
    head = lax.slice_in_dim(cells, 0, 2, axis=dim)
    tail = lax.slice_in_dim(cells, cells.shape[dim] - 2, cells.shape[dim], axis=dim)
    before = lax.ppermute(tail, axis, [(i, (i + 1) % count) for i in range(count)])
    after = lax.ppermute(head, axis, [((i + 1) % count, i) for i in range(count)])
    return before, after


def per_device(modes, adv_index):
    cells_x, cells_y, cells_z, components, width = modes.shape
    advecting = adv_index.shape[0]
    groups_x = lax.axis_size("gx")
    groups_y = lax.axis_size("gy")
    order = (3, 2, 0, 1, 4)
    before_x, after_x = neighbours(modes, "gx", 0)
    before_y, after_y = neighbours(modes, "gy", 1)
    gap = jnp.zeros((cells_x, 4, cells_z, components, width), modes.dtype)
    rim = jnp.concatenate([after_y, gap, before_y], axis=1)
    columns = jnp.pad(adv_index, (0, LANES - advecting), constant_values=-1)
    pick = (lax.broadcasted_iota(jnp.int32, (width, LANES), 0) == columns[None, :]).astype(jnp.bfloat16)
    partial = convect(
        jnp.transpose(modes, order),
        jnp.transpose(before_x, order),
        jnp.transpose(after_x, order),
        jnp.transpose(rim, order),
        pick,
        advecting,
        groups_x,
    )
    high, wide = width // groups_x, width // groups_y
    parts = lax.all_to_all(partial, "gx", 0, 0, tiled=True)
    owned = jnp.sum(parts.astype(jnp.float32), axis=0).astype(jnp.bfloat16)
    owned = jnp.transpose(owned.reshape(high, advecting, groups_y, wide), (2, 0, 1, 3))
    owned = lax.all_to_all(owned.reshape(groups_y, high, advecting * wide), "gy", 0, 0, tiled=True)
    total = jnp.sum(owned.astype(jnp.float32), axis=0)
    factor = 1.0 / math.sqrt(3.0 * cells_x * cells_y * cells_z * groups_x * groups_y)
    return total.reshape(high, advecting, wide) * factor


def solution(mesh):
    return jax.shard_map(
        per_device,
        mesh=mesh,
        in_specs=(P("gx", "gy", None, None, None), P()),
        out_specs=P("gx", None, "gy"),
        check_vma=False,
    )
```

time: 370 us -> 106 us (0.29)
  other arithmetic: 124 us -> 1.12 us
  local copies, waits for them, and re-layouts: 112 us -> 11.4 us
  waiting for transfers between devices: 79.5 us -> 3.99 us
  Pallas kernels: 0 us -> 54.4 us
  matrix products: 30.8 us -> 0 us
  blocking collectives: 0 us -> 26.8 us
  between operations: 14.2 us -> 0.17 us
    convert_element_type x4 -> x1, other arithmetic: 107 us -> 0.02 us  [per_device(): (lax.broadcasted_iota(jnp.int32, (width, LANES), 0) == columns[None, :])....]
    unnamed x4 -> x0, waiting for transfers between devices: 55.3 us -> none
    pallas_call x0 -> x2, Pallas kernels: none -> 54.4 us  [the longest x1 48.9 us: convect(): pl.pallas_call(functools.partial(kernel, advecting), out_shape=jax.ShapeD...]
    unnamed x59 -> x15, local copies, waits for them, and re-layouts: 59.4 us -> 7.14 us
    mul x26 -> x1, local copies, waits for them, and re-layouts: 35.2 us -> 0.74 us  [per_device(): return total.reshape(high, advecting, wide) * factor]
    dot_general x8 -> x0, matrix products: 30.8 us -> none  [convect(): lax.dot_general(flat, field, (((0,), (0,)), ((), ())), preferred_element_...]
    all_to_all x0 -> x2, blocking collectives: none -> 26.8 us  [the longest x1 17.9 us: per_device(): parts = lax.all_to_all(partial, 'gx', 0, 0, tiled=True)]
    reduce_scatter x2 -> x0, waiting for transfers between devices: 24.1 us -> none  [per_device(): lax.psum_scatter(partial_value, 'gy', scatter_dimension=2, tiled=True)]
  transfers between devices with their start and end apart: 7 -> 4, of which waited for: 2 -> 1; matrix products, arithmetic and copies ran while one was open for 37% -> 4% of each run, Pallas kernels for 0% -> 5%
where the time goes in v1:
time: 106 us
  Pallas kernels  54.4 us (51%)
  blocking collectives  26.8 us (25%)
  local copies, waits for them, and re-layouts  11.4 us (11%)
  starting transfers between devices  7.95 us (8%)
  waiting for transfers between devices  3.99 us (4%)
  other arithmetic  1.12 us (1%)
    pallas_call x1, Pallas kernels, convect(): pl.pallas_call(functools.partial(kernel, advecting), out_shape=jax.ShapeD...  48.9 us
    all_to_all x1, blocking collectives, per_device(): parts = lax.all_to_all(partial, 'gx', 0, 0, tiled=True)  17.9 us
    all_to_all x1, blocking collectives, per_device(): lax.all_to_all(owned.reshape(groups_y, high, advecting * wide), 'gy', 0,...  8.93 us
    unnamed x15, local copies, waits for them, and re-layouts  7.14 us
    pallas_call x1, Pallas kernels, convect(): pl.pallas_call(prepare, out_shape=[jax.ShapeDtypeStruct((blocks, width, c...  5.53 us
    ppermute x2, starting transfers between devices, neighbours(): lax.ppermute(head, axis, [((i + 1) % count, i) for i in range(count)])  5.03 us
    ppermute x2, waiting for transfers between devices, neighbours(): lax.ppermute(head, axis, [((i + 1) % count, i) for i in range(count)])  3.98 us
    slice x2, local copies, waits for them, and re-layouts, neighbours(): head = lax.slice_in_dim(cells, 0, 2, axis=dim)  2.93 us
  transfers between devices with their start and end apart: 4, of which 1 were waited for; matrix products, arithmetic and copies ran while one was open for 4% of the time, Pallas kernels for 5%

profile of v1, /device:TPU:0, one launch (start us, length us, event | category | flops | bytes accessed | tf_op | source)
XLA Modules:
  0.0 105.8 jit_solution(520289020744397298)
XLA Ops:
  0.0 0.0 copy-start.3
  0.0 1.5 %fusion.2 = (bf16[2,32,4,3,256]{4,2,3,1,0:T(4,128)(2,1)S(1)}, bf16[2,32,4,3,256]{4,2,3,1,0:T(4,128)(2,1)S(1)}) fusion(bf16[32,32,4,3,256]{4,2,3,1,0:T(4,128)(2,1)} %param.2), kind=kLoop, calls=%fused_computation.7 | loop fusion | bytes 1572864 | tf_op jit(solution)/shard_map/slice | solution.py:139
  1.5 0.1 copy.20
  1.6 0.5 collective-permute-start
  2.2 2.9 %collective-permute-start.1 = (bf16[2,32,4,3,256]{4,1,0,2,3:T(8,128)(2,1)S(1)}, bf16[2,32,4,3,256]{4,1,0,2,3:T(8,128)(2,1)S(1)}, u32[]{:S(2)}, u32[]{:S(2)}) collective-permute-start(bf16[2,32,4,3,256]{4,1,0,2,3:T(8,128)(2,1)S(1)} %copy.21), channel_id=1, source_target_pairs={{4,0},{8,4},{12,8},{16,12},{20,16},{24,20},{28,24},{0,28},{5,1},{9... | collective-permute-start | bytes 1179656 | tf_op jit(solution)/shard_map/ppermute | solution.py:142
  5.1 1.4 %fusion.1 = (bf16[32,2,4,3,256]{4,2,3,1,0:T(4,128)(2,1)S(1)}, bf16[32,2,4,3,256]{4,2,3,1,0:T(4,128)(2,1)S(1)}) fusion(bf16[32,32,4,3,256]{4,2,3,1,0:T(4,128)(2,1)} %param.2), kind=kLoop, calls=%fused_computation.6 | loop fusion | bytes 1572864 | tf_op jit(solution)/shard_map/slice | solution.py:139
  6.5 0.3 copy.22
  6.8 2.4 %collective-permute-start.3 = (bf16[32,2,4,3,256]{4,1,0,2,3:T(2,128)(2,1)S(1)}, bf16[32,2,4,3,256]{4,1,0,2,3:T(2,128)(2,1)S(1)}, u32[]{:S(2)}, u32[]{:S(2)}) collective-permute-start(bf16[32,2,4,3,256]{4,1,0,2,3:T(2,128)(2,1)S(1)} %copy.22), channel_id=1, source_target_pairs={{0,1},{1,2},{2,3},{3,0},{4,5},{5,6},{6,7},{7,4},{8,9},{9,10},{10,1... | collective-permute-start | bytes 1179656 | tf_op jit(solution)/shard_map/ppermute | solution.py:141
  9.2 0.3 copy.23
  9.5 0.0 copy-start.4
  9.5 2.1 %collective-permute-start.2 = (bf16[32,2,4,3,256]{4,1,0,2,3:T(2,128)(2,1)S(1)}, bf16[32,2,4,3,256]{4,1,0,2,3:T(2,128)(2,1)S(1)}, u32[]{:S(2)}, u32[]{:S(2)}) collective-permute-start(bf16[32,2,4,3,256]{4,1,0,2,3:T(2,128)(2,1)S(1)} %copy.23), channel_id=1, source_target_pairs={{1,0},{2,1},{3,2},{0,3},{5,4},{6,5},{7,6},{4,7},{9,8},{10,9},{11,1... | collective-permute-start | bytes 1179656 | tf_op jit(solution)/shard_map/ppermute | solution.py:142
  11.6 0.0 copy-done.3
  11.6 1.2 %copy.24 = bf16[32,32,4,3,256]{4,1,0,2,3:T(8,128)(2,1)S(1)} copy(bf16[32,32,4,3,256]{4,2,3,1,0:T(4,128)(2,1)S(1)} %copy-done.3) | data formatting | bytes 12582912 | tf_op args[0]
  12.8 0.0 copy-done.4
  12.8 0.0 copy-start
  12.9 5.5 %prepare.1 = (bf16[16,256,768]{2,1,0:T(8,128)(2,1)S(1)}, bf16[16,3,256,128]{3,2,1,0:T(8,128)(2,1)S(1)}, bf16[16,3,256,256]{3,2,1,0:T(8,128)(2,1)S(1)}) custom-call(bf16[3,4,32,32,256]{4,3,2,1,0:T(8,128)(2,1)S(1)} %bitcast.10, bf16[256,128]{1,0:T(8,128)(2,1)S(1)} %fusion.pick_ref), custom_call_target="tpu_custom_call" | custom-call | flops 20000000000 | bytes 30000000 | tf_op jit(solution)/shard_map/prepare/pallas_call | solution.py:108
  18.4 0.0 copy-done
  18.4 0.0 copy-start.1
  18.4 2.6 %copy-done.1 = bf16[16,256,768]{2,1,0:T(8,128)(2,1)} copy-done((bf16[16,256,768]{2,1,0:T(8,128)(2,1)}, bf16[16,256,768]{2,1,0:T(8,128)(2,1)S(1)}, u32[]{:S(2)}) %copy-start.1) | copy-done | bytes 6291480
  21.1 0.0 copy-start.2
  21.1 2.6 %copy-done.2 = bf16[16,3,256,256]{3,2,1,0:T(8,128)(2,1)} copy-done((bf16[16,3,256,256]{3,2,1,0:T(8,128)(2,1)}, bf16[16,3,256,256]{3,2,1,0:T(8,128)(2,1)S(1)}, u32[]{:S(2)}) %copy-start.2) | copy-done | bytes 6291480
  23.7 0.1 pad.6.clone
  23.8 0.0 collective-permute-done.3
  23.8 4.0 %collective-permute-done.2 = bf16[32,2,4,3,256]{4,1,0,2,3:T(2,128)(2,1)S(1)} collective-permute-done((bf16[32,2,4,3,256]{4,1,0,2,3:T(2,128)(2,1)S(1)}, bf16[32,2,4,3,256]{4,1,0,2,3:T(2,128)(2,1)S(1)}, u32[]{:S(2)}, u32[]{:S(2)}) %collective-permute-start.2) | collective-permute-done | bytes 393248 | tf_op jit(solution)/shard_map/ppermute | solution.py:142
  27.7 0.9 maximum_bitcast_fusion.yh_ref
  28.7 0.0 collective-permute-done
  28.7 0.0 collective-permute-done.1
  28.7 48.9 %convect.1 = bf16[8,32,2048]{2,1,0:T(8,128)(2,1)S(1)} custom-call(bf16[3,4,32,32,256]{4,3,2,1,0:T(8,128)(2,1)} %bitcast.11, bf16[3,4,2,32,256]{4,3,2,1,0:T(8,128)(2,1)S(1)} %bitcast.12, bf16[3,4,2,32,256]{4,3,2,1,0:T(8,128)(2,1)S(1)} %bitcast.13, bf16[3,4,32,8,256]{4,3,2,1,0:T(8,128)(2,1)S(1)} %maximum_bitcast_fusion.yh_ref, ...), custom_call_target="tpu_custom_call" | custom-call | tf_op jit(solution)/shard_map/convect/pallas_call | solution.py:122
  77.6 17.9 %all_to_all.10 = bf16[8,32,2048]{2,1,0:T(8,128)(2,1)S(1)} all-to-all(bf16[8,32,2048]{2,1,0:T(8,128)(2,1)S(1)} %convect.1), channel_id=1, replica_groups=mesh['gx'=8,'gy'=4] {'gx'}, dimensions={0} | all-to-all | bytes 2097152 | tf_op jit(solution)/shard_map/all_to_all | solution.py:168
  95.5 0.1 reduce_sum.21
  95.6 0.2 reshape.10
  95.9 0.2 reshape.11
  96.1 8.9 %all_to_all.11 = bf16[4,32,512]{2,1,0:T(8,128)(2,1)S(1)} all-to-all(bf16[4,32,512]{2,1,0:T(8,128)(2,1)S(1)} %reshape.11), channel_id=1, replica_groups=mesh['gx'=8,'gy'=4] {'gy'}, dimensions={0} | all-to-all | bytes 262144 | tf_op jit(solution)/shard_map/all_to_all | solution.py:171
  105.1 0.7 mul.11
  (7 shorter events, 0.1 us)
Async XLA Ops:
  0.0 11.6 %copy-start.3 = (bf16[32,32,4,3,256]{4,2,3,1,0:T(4,128)(2,1)S(1)}, bf16[32,32,4,3,256]{4,2,3,1,0:T(4,128)(2,1)}, u32[]{:S(2)}) copy-start(bf16[32,32,4,3,256]{4,2,3,1,0:T(4,128)(2,1)} %param.2) | copy-start | bytes 18874372
  1.6 27.1 %collective-permute-start = (bf16[2,32,4,3,256]{4,1,0,2,3:T(8,128)(2,1)S(1)}, bf16[2,32,4,3,256]{4,1,0,2,3:T(8,128)(2,1)S(1)}, u32[]{:S(2)}, u32[]{:S(2)}) collective-permute-start(bf16[2,32,4,3,256]{4,1,0,2,3:T(8,128)(2,1)S(1)} %copy.20), channel_id=1, source_target_pairs={{0,4},{4,8},{8,12},{12,16},{16,20},{20,24},{24,28},{28,0},{1,5},{5... | collective-permute-start | bytes 1179656 | tf_op jit(solution)/shard_map/ppermute | solution.py:141
  2.2 26.5 %collective-permute-start.1 = (bf16[2,32,4,3,256]{4,1,0,2,3:T(8,128)(2,1)S(1)}, bf16[2,32,4,3,256]{4,1,0,2,3:T(8,128)(2,1)S(1)}, u32[]{:S(2)}, u32[]{:S(2)}) collective-permute-start(bf16[2,32,4,3,256]{4,1,0,2,3:T(8,128)(2,1)S(1)} %copy.21), channel_id=1, source_target_pairs={{4,0},{8,4},{12,8},{16,12},{20,16},{24,20},{28,24},{0,28},{5,1},{9... | collective-permute-start | bytes 1179656 | tf_op jit(solution)/shard_map/ppermute | solution.py:142
  6.8 16.9 %collective-permute-start.3 = (bf16[32,2,4,3,256]{4,1,0,2,3:T(2,128)(2,1)S(1)}, bf16[32,2,4,3,256]{4,1,0,2,3:T(2,128)(2,1)S(1)}, u32[]{:S(2)}, u32[]{:S(2)}) collective-permute-start(bf16[32,2,4,3,256]{4,1,0,2,3:T(2,128)(2,1)S(1)} %copy.22), channel_id=1, source_target_pairs={{0,1},{1,2},{2,3},{3,0},{4,5},{5,6},{6,7},{7,4},{8,9},{9,10},{10,1... | collective-permute-start | bytes 1179656 | tf_op jit(solution)/shard_map/ppermute | solution.py:141
  9.5 3.3 %copy-start.4 = (s32[8]{0:T(128)S(1)}, s32[8]{0:T(128)}, u32[]{:S(2)}) copy-start(s32[8]{0:T(128)} %param.3) | copy-start | bytes 100
  9.5 18.2 %collective-permute-start.2 = (bf16[32,2,4,3,256]{4,1,0,2,3:T(2,128)(2,1)S(1)}, bf16[32,2,4,3,256]{4,1,0,2,3:T(2,128)(2,1)S(1)}, u32[]{:S(2)}, u32[]{:S(2)}) collective-permute-start(bf16[32,2,4,3,256]{4,1,0,2,3:T(2,128)(2,1)S(1)} %copy.23), channel_id=1, source_target_pairs={{1,0},{2,1},{3,2},{0,3},{5,4},{6,5},{7,6},{4,7},{9,8},{10,9},{11,1... | collective-permute-start | bytes 1179656 | tf_op jit(solution)/shard_map/ppermute | solution.py:142
  12.8 5.6 %copy-start = (bf16[32,32,4,3,256]{4,1,0,2,3:T(8,128)(2,1)}, bf16[32,32,4,3,256]{4,1,0,2,3:T(8,128)(2,1)S(1)}, u32[]{:S(2)}) copy-start(bf16[32,32,4,3,256]{4,1,0,2,3:T(8,128)(2,1)S(1)} %copy.24) | copy-start | bytes 18874372
  18.4 2.6 %copy-start.1 = (bf16[16,256,768]{2,1,0:T(8,128)(2,1)}, bf16[16,256,768]{2,1,0:T(8,128)(2,1)S(1)}, u32[]{:S(2)}) copy-start(bf16[16,256,768]{2,1,0:T(8,128)(2,1)S(1)} %get-tuple-element.8.turned_ref) | copy-start | bytes 18874372
  21.1 2.6 %copy-start.2 = (bf16[16,3,256,256]{3,2,1,0:T(8,128)(2,1)}, bf16[16,3,256,256]{3,2,1,0:T(8,128)(2,1)S(1)}, u32[]{:S(2)}) copy-start(bf16[16,3,256,256]{3,2,1,0:T(8,128)(2,1)S(1)} %get-tuple-element.10.ahead_ref) | copy-start | bytes 18874372
